TPU v7x, 256 devices: a whole 4x4x8 slice. The times are simulated.
256 devices in a mesh: dp: 64 (over x, z_hi, y), mp: 4 (over z_lo, core).
Axes of the slice: x: 4, y: 4, z: 8 (z_hi: 4, z_lo: 2; z = z_hi * 2 + z_lo), core: 2. Of those that a mesh axis runs over, the one named last changes fastest.
Arguments:
- history_sequences: float32 [512, 512], P('dp'), may hold values from -65 to 65, as said below
- later_steps: float32 [512, 128], P('dp'), may hold values from -65 to 65
- patch_lift_matrix: bfloat16 [32, 1280], P(None, 'dp'), may hold values from -1 to 1
- scaling_factors: bfloat16 [2, 1280], P(None, 'dp'), may hold values from 0.5 to 1.5
- asking_matrix: bfloat16 [1280, 1280], P('dp', 'mp'), may hold values from -0.15625 to 0.15625
- lookup_matrix: bfloat16 [1280, 1280], P('dp', 'mp'), may hold values from -0.15625 to 0.15625
- content_matrix: bfloat16 [1280, 1280], P('dp', 'mp'), may hold values from -0.15625 to 0.15625
- attend_exit_matrix: bfloat16 [1280, 1280], P('mp', 'dp'), may hold values from -0.15625 to 0.15625
- outlook_matrix: bfloat16 [1280, 1280], P('dp', 'mp'), may hold values from -0.15625 to 0.15625
Outputs:
- loss_mean: float32 [], replicated
- embed_grad: float32 [32, 1280], P(None, 'dp')
- gains_grad: float32 [2, 1280], P(None, 'dp')
- query_grad: float32 [1280, 1280], P('dp', 'mp')
- key_grad: float32 [1280, 1280], P('dp', 'mp')
- value_grad: float32 [1280, 1280], P('dp', 'mp')
- output_grad: float32 [1280, 1280], P('mp', 'dp')
- head_weight_gradient: float32 [1280, 1280], P('dp', 'mp')
Inputs may be any that keep to these rules, and one draw needn't show every extreme that they name: `history_sequences`: later_steps continues the history of each series.
All inputs are finite; a program needn't handle non-finite values.
Results may differ from a plain program's by a relative error of at most 0.005.
Values may be sent and summed in bfloat16 or wider, within the bound.
No kernel may reach another device: no remote copies, remote signals or barrier semaphores. Data moves between devices by JAX's collectives and lax.ppermute only.
A program may use at most 64 MiB of HBM per device.

v0:
```python
import math
import jax
import jax.numpy as jnp
from jax import lax
from jax.sharding import Mesh
from jax.sharding import PartitionSpec as P

PATCH = 32
HORIZON_SPAN = 128
PATCHES = 16
LEVEL_CHANNELS = 10
HEAD_DIM = 80
DP = ("dp_0", "dp_1", "dp_2")
MP = ("mp_0", "mp_1")
DP_MP = ("dp_0", "dp_1", "dp_2", "mp_0", "mp_1")
EPS = 1e-06
STAT_EPS = 1e-05
SMOOTHING_RADIUS = 0.05


def gather_turned(arrays, axis, dims):
    turned = [jnp.moveaxis(a, dim, 0) for a, dim in zip(arrays, dims)]
    both = jnp.concatenate([t.reshape(len(t), -1) for t in turned], axis=1)
    out, at, outs = (lax.all_gather(both, axis, axis=0, tiled=True), 0, [])
    for t, dim in zip(turned, dims):
        piece = out[:, at : at + t[0].size].reshape(-1, *t.shape[1:])
        outs.append(jnp.moveaxis(piece, 0, dim))
        at += t[0].size
    return tuple(outs)


def in_one_piece(arrays, axis, dim, along):
    ends, at = ([], 0)
    for a in arrays[:-1]:
        at += a.shape[along]
        ends.append(at)
    both = jnp.concatenate(arrays, axis=along)
    return tuple(jnp.split(lax.all_gather(both, axis, axis=dim, tiled=True), ends, axis=along))


def from_everyone(x, axis):
    length = lax.axis_size(axis)
    return lax.all_to_all(jnp.broadcast_to(x[None], (length, *x.shape)), axis, 0, 0, tiled=True)


def over_copies(x, axis):
    return from_everyone(x, axis).sum(axis=0)


def by_axis(x, axes):
    for axis in axes:
        x = lax.psum(x, axis)
    return x


def taken_together(x, axis):
    return from_everyone(x, axis).astype(jnp.float32).sum(axis=0)


def split_up(x, dim, length):
    before, after = (x.shape[:dim], x.shape[dim + 1 :])
    return jnp.moveaxis(x.reshape(*before, length, -1, *after), dim, 0)


def sum_at_owner(x, axis, dim):
    length = lax.axis_size(axis)
    tiles = lax.all_to_all(split_up(x, dim, length), axis, 0, 0, tiled=True)
    return jnp.sum(tiles.astype(jnp.float32), axis=0)


def sent_together(arrays, axis, dim, along):
    ends, at = ([], 0)
    for a in arrays[:-1]:
        at += a.shape[along]
        ends.append(at)
    both = jnp.concatenate(arrays, axis=along)
    return tuple(jnp.split(sum_at_owner(both, axis, dim), ends, axis=along))


def summed_on_arrival(x, axis, dim):
    tiles = split_up(x, dim, lax.axis_size(axis))
    arrived = lax.all_to_all(tiles, axis, split_axis=0, concat_axis=0, tiled=True)
    return arrived.sum(axis=0)


def sent_together_2(arrays, axis, dim, along):
    both = jnp.concatenate(arrays, axis=along)
    out, at, outs = (summed_on_arrival(both, axis, dim), 0, [])
    for a in arrays:
        outs.append(lax.slice_in_dim(out, at, at + a.shape[along], axis=along))
        at += a.shape[along]
    return tuple(outs)


def rms_forward(residual, gain):
    factor = lax.rsqrt(jnp.mean(residual * residual, axis=1, keepdims=True) + EPS)
    return ((residual * factor * gain[None, :]).astype(jnp.bfloat16), factor)


def rms_backward(residual, factor, gain, upstream):
    weighted = gain[None, :] * upstream
    inner = jnp.mean(weighted * residual, axis=1, keepdims=True)
    back = factor * weighted - residual * factor * factor * factor * inner
    gain_term = jnp.sum(upstream * residual * factor, axis=0)
    return (back, gain_term)


def positions(length, width):
    half = width // 2
    freqs = jnp.exp(-math.log(10000.0) * jnp.arange(half, dtype=jnp.float32) / half)
    angles = jnp.arange(length, dtype=jnp.float32)[:, None] * freqs[None, :]
    return jnp.concatenate([jnp.sin(angles), jnp.cos(angles)], axis=1)


def prepare(history_sequences, later_steps):
    number = history_sequences.shape[0]
    centre = jnp.mean(history_sequences, axis=1, keepdims=True)
    spread = jnp.sqrt(
        jnp.mean((history_sequences - centre) * (history_sequences - centre), axis=1, keepdims=True)
        + STAT_EPS
    )
    normed = (history_sequences - centre) / spread
    ahead = (later_steps - centre) / spread
    joined = jnp.concatenate([normed, ahead], axis=1).reshape(number, -1, PATCH)
    reach = later_steps.shape[1] // PATCH
    future_values = jnp.concatenate(
        [joined[:, offset + 1 : offset + 1 + PATCHES] for offset in range(reach)], axis=2
    )
    future_values = future_values.reshape(number * PATCHES, reach * PATCH)
    patches = normed.reshape(number * PATCHES, PATCH).astype(jnp.bfloat16)
    return (patches, future_values)


def attention_forward(queries, keys, values, number):
    layout = (number, PATCHES, -1, HEAD_DIM)
    query_blocks = queries.reshape(layout)
    key_blocks = keys.reshape(layout)
    value_blocks = values.reshape(layout)
    scale = 1.0 / math.sqrt(HEAD_DIM)
    scores = (
        jnp.einsum("sihd,sjhd->shij", query_blocks, key_blocks, preferred_element_type=jnp.float32)
        * scale
    )
    place = jnp.arange(PATCHES)
    causal = place[:, None] >= place[None, :]
    raised = jnp.where(causal, jnp.exp(scores), 0.0)
    probs = raised / jnp.sum(raised, axis=3, keepdims=True)
    probs_low = probs.astype(jnp.bfloat16)
    context = jnp.einsum(
        "shij,sjhd->sihd", probs_low, value_blocks, preferred_element_type=jnp.float32
    )
    context = context.astype(jnp.bfloat16).reshape(number * PATCHES, -1)
    return (context, probs, probs_low)


def attention_backward(context_grad, queries, keys, values, probs, probs_low, number):
    layout = (number, PATCHES, -1, HEAD_DIM)
    query_blocks = queries.reshape(layout)
    key_blocks = keys.reshape(layout)
    value_blocks = values.reshape(layout)
    grad_blocks = context_grad.reshape(layout)
    scale = 1.0 / math.sqrt(HEAD_DIM)
    prob_grad = jnp.einsum(
        "sihd,sjhd->shij", grad_blocks, value_blocks, preferred_element_type=jnp.float32
    )
    value_back = jnp.einsum(
        "shij,sihd->sjhd", probs_low, grad_blocks, preferred_element_type=jnp.float32
    ).astype(jnp.bfloat16)
    centred = prob_grad - jnp.sum(probs * prob_grad, axis=3, keepdims=True)
    score_grad = (probs * centred * scale).astype(jnp.bfloat16)
    query_back = jnp.einsum(
        "shij,sjhd->sihd", score_grad, key_blocks, preferred_element_type=jnp.float32
    ).astype(jnp.bfloat16)
    key_back = jnp.einsum(
        "shij,sihd->sjhd", score_grad, query_blocks, preferred_element_type=jnp.float32
    ).astype(jnp.bfloat16)
    flat = (number * PATCHES, -1)
    return (query_back.reshape(flat), key_back.reshape(flat), value_back.reshape(flat))


def pinball_terms(estimate_entries, actual_entries):
    batch_example_tally = estimate_entries.shape[0]
    horizon_error = actual_entries[:, :, None] - estimate_entries.reshape(
        batch_example_tally, -1, LEVEL_CHANNELS
    )
    cumulative_share = jnp.arange(LEVEL_CHANNELS, dtype=jnp.float32) / LEVEL_CHANNELS
    mean_indicator = jnp.arange(LEVEL_CHANNELS) == 0
    lopsided_errors = jnp.where(
        mean_indicator,
        horizon_error * horizon_error,
        cumulative_share * horizon_error
        + SMOOTHING_RADIUS * jax.nn.softplus(-horizon_error / SMOOTHING_RADIUS),
    )
    skew_coefficient = (
        jnp.where(
            mean_indicator,
            -2.0 * horizon_error,
            jax.nn.sigmoid(-horizon_error / SMOOTHING_RADIUS) - cumulative_share,
        )
        / HORIZON_SPAN
    )
    return (
        jnp.sum(lopsided_errors) / HORIZON_SPAN,
        skew_coefficient.reshape(batch_example_tally, -1).astype(jnp.bfloat16),
    )


def multiplied_rows(left, right):

    def term(start, count):
        return jnp.dot(left, right, preferred_element_type=jnp.float32)

    return term


def per_device(
    history_sequences,
    later_steps,
    patch_lift_matrix,
    scaling_factors,
    asking_matrix,
    lookup_matrix,
    content_matrix,
    attend_exit_matrix,
    outlook_matrix,
):
    number = history_sequences.shape[0]
    rows_all = number * PATCHES
    patches, future_values = prepare(history_sequences, later_steps)
    embed_full, gains_full = gather_turned((patch_lift_matrix, scaling_factors), DP, (1, 1))
    gains = gains_full.astype(jnp.float32)
    query_full, key_full, value_full, outlook_collected = in_one_piece(
        (asking_matrix, lookup_matrix, content_matrix, outlook_matrix), DP, 0, 1
    )
    output_full = lax.all_gather(attend_exit_matrix, DP, axis=1, tiled=True)
    residual_zero = jnp.dot(patches, embed_full, preferred_element_type=jnp.float32) + jnp.tile(
        positions(PATCHES, embed_full.shape[1]), (number, 1)
    )
    normed_attn, factor_attn = rms_forward(residual_zero, gains[0])
    queries = jnp.dot(normed_attn, query_full, preferred_element_type=jnp.float32).astype(
        jnp.bfloat16
    )
    keys = jnp.dot(normed_attn, key_full, preferred_element_type=jnp.float32).astype(jnp.bfloat16)
    values = jnp.dot(normed_attn, value_full, preferred_element_type=jnp.float32).astype(
        jnp.bfloat16
    )
    context, probs, probs_low = attention_forward(queries, keys, values, number)
    attn_term = multiplied_rows(context, output_full)
    residual_one = residual_zero + over_copies(attn_term(0, rows_all), MP)
    normed_head, factor_head = rms_forward(residual_one, gains[1])
    estimate_entries = jnp.dot(normed_head, outlook_collected, preferred_element_type=jnp.float32)
    device_portion = estimate_entries.shape[1] // LEVEL_CHANNELS
    actual_entries = lax.dynamic_slice_in_dim(
        future_values, lax.axis_index(MP) * device_portion, device_portion, 1
    )
    device_loss, estimate_derivative = pinball_terms(estimate_entries, actual_entries)
    total_loss_value = by_axis(device_loss, DP_MP)
    loss_mean = total_loss_value / (number * PATCHES * lax.axis_size(DP))
    head_weight_gradient = jnp.dot(
        normed_head.T, estimate_derivative, preferred_element_type=jnp.float32
    )
    head_contribution = multiplied_rows(estimate_derivative, outlook_collected.T)
    head_reverse = taken_together(head_contribution(0, rows_all).astype(jnp.bfloat16), MP).astype(
        jnp.float32
    )
    residual_one_grad, gain_one = rms_backward(residual_one, factor_head, gains[1], head_reverse)
    attn_low = residual_one_grad.astype(jnp.bfloat16)
    output_grad = jnp.dot(context.T, attn_low, preferred_element_type=jnp.float32)
    context_grad = jnp.dot(attn_low, output_full.T, preferred_element_type=jnp.float32).astype(
        jnp.bfloat16
    )
    query_back, key_back, value_back = attention_backward(
        context_grad, queries, keys, values, probs, probs_low, number
    )
    query_grad = jnp.dot(normed_attn.T, query_back, preferred_element_type=jnp.float32)
    key_grad = jnp.dot(normed_attn.T, key_back, preferred_element_type=jnp.float32)
    value_grad = jnp.dot(normed_attn.T, value_back, preferred_element_type=jnp.float32)
    total = jnp.dot(query_back, query_full.T, preferred_element_type=jnp.float32)
    total = total + jnp.dot(key_back, key_full.T, preferred_element_type=jnp.float32)
    attn_back = taken_together(
        (total + jnp.dot(value_back, value_full.T, preferred_element_type=jnp.float32)).astype(
            jnp.bfloat16
        ),
        MP,
    ).astype(jnp.float32)
    norm_back_zero, gain_zero = rms_backward(residual_zero, factor_attn, gains[0], attn_back)
    residual_zero_grad = residual_one_grad + norm_back_zero
    embed_grad = jnp.dot(
        patches.T, residual_zero_grad.astype(jnp.bfloat16), preferred_element_type=jnp.float32
    )
    gains_grad = jnp.stack([gain_zero, gain_one], axis=0)
    query_grad, key_grad, value_grad, head_weight_gradient = sent_together(
        (
            query_grad.astype(jnp.bfloat16),
            key_grad.astype(jnp.bfloat16),
            value_grad.astype(jnp.bfloat16),
            head_weight_gradient.astype(jnp.bfloat16),
        ),
        DP,
        0,
        1,
    )
    output_grad = sum_at_owner(output_grad.astype(jnp.bfloat16), DP, 1)
    embed_grad, gains_grad = sent_together_2((embed_grad, gains_grad), DP, 1, 0)
    return (
        loss_mean,
        embed_grad,
        gains_grad,
        query_grad,
        key_grad,
        value_grad,
        output_grad,
        head_weight_gradient,
    )


def solution(mesh):
    split = Mesh(mesh.devices.reshape(4, 4, 4, 2, 2), ("dp_0", "dp_1", "dp_2", "mp_0", "mp_1"))
    placed = (
        P(DP, None),
        P(DP, None),
        P(None, DP),
        P(None, DP),
        P(DP, MP),
        P(DP, MP),
        P(DP, MP),
        P(MP, DP),
        P(DP, MP),
    )
    return jax.shard_map(
        per_device,
        mesh=split,
        in_specs=placed,
        out_specs=(
            P(),
            P(None, DP),
            P(None, DP),
            P(DP, MP),
            P(DP, MP),
            P(DP, MP),
            P(MP, DP),
            P(DP, MP),
        ),
        check_vma=False,
    )
```

profile of v0, /device:TPU:1, one launch (start us, length us, event | category | flops | bytes accessed | tf_op | source)
XLA Modules:
  0.0 718.7 jit_solution(1902449885133331667)
XLA Ops:
  7.2 1.5 concatenate.30
  12.9 172.1 %all-gather = bf16[64,20,34]{2,1,0:T(8,128)(2,1)S(1)} all-gather(bf16[1,20,34]{2,1,0:T(8,128)(2,1)S(1)} %maximum_bitcast_fusion.1), channel_id=1, replica_groups=mesh['dp_0'=4,'dp_1'=4,'dp_2'=4,'mp_0'=2,'mp_1'=2] {'dp_0','dp_1','dp_2'}, dimensions={0}, use_global_device_ids=true | all-gather | bytes 88400 | tf_op jit(solution)/shard_map/all_gather | solution.py:24
  185.5 164.7 %all-gather.2 = bf16[64,20,320]{2,1,0:T(8,128)(2,1)S(1)} all-gather(bf16[1,20,320]{2,1,0:T(8,128)(2,1)} %bitcast.63), channel_id=1, replica_groups=mesh['dp_0'=4,'dp_1'=4,'dp_2'=4,'mp_0'=2,'mp_1'=2] {'dp_0','dp_1','dp_2'}, dimensions={0}, use_global_device_ids=true | all-gather | bytes 832000 | tf_op jit(solution)/shard_map/all_gather | solution.py:235
  351.5 6.2 reshape.143
  357.7 1.7 convolution_convert_fusion.13
  359.4 2.3 convolution_convert_fusion.11
  361.7 1.7 convolution_convert_fusion.12
  365.4 1.7 broadcast_in_dim.61
  367.1 57.9 %all-to-all-start = ((f32[4,128,1280]{2,1,0:T(8,128)}), f32[4,128,1280]{2,1,0:T(8,128)S(1)}, u32[]{:S(2)}, u32[]{:S(2)}) async-start(f32[4,128,1280]{2,1,0:T(8,128)} %broadcast_in_dim.61), calls=%async_computation | async-start | bytes 5242880 | tf_op jit(solution)/shard_map/all_to_all | solution.py:43
  428.8 26.1 %all-to-all-done = f32[4,128,1280]{2,1,0:T(8,128)S(1)} async-done(((f32[4,128,1280]{2,1,0:T(8,128)}), f32[4,128,1280]{2,1,0:T(8,128)S(1)}, u32[]{:S(2)}, u32[]{:S(2)}) %all-to-all-start) | async-done | bytes 2621472 | tf_op jit(solution)/shard_map/all_to_all | solution.py:43
  456.0 1.2 multiply_reduce_fusion.4
  457.3 2.9 fusion.32
  460.2 2.1 convolution_convert_fusion.5
  462.2 1.2 broadcast_in_dim.62
  463.4 5.5 all-to-all-start.1
  469.7 15.6 %all-to-all-done.1 = bf16[4,128,1280]{2,1,0:T(8,128)(2,1)} async-done(((bf16[4,128,1280]{2,1,0:T(8,128)(2,1)}), bf16[4,128,1280]{2,1,0:T(8,128)(2,1)}, u32[]{:S(2)}, u32[]{:S(2)}) %all-to-all-start.1) | async-done | bytes 1310752 | tf_op jit(solution)/shard_map/all_to_all | solution.py:43
  485.3 1.6 convert_reduce_fusion.2
  488.4 1.3 fusion.9
  489.7 1.3 fusion.10
  490.9 1.2 fusion.11
  492.4 1.7 fusion.16
  494.5 1.9 convolution_add_fusion.1
  496.4 1.6 fusion.1
  499.1 4.7 all-to-all-start.2
  503.8 2.3 convolution_convert_fusion
  506.3 2.2 convolution_convert_fusion.1
  508.5 2.2 copy.121
  510.7 2.2 reshape.139
  512.9 1.3 convolution_convert_fusion.2
  514.3 1.3 convolution_convert_fusion.3
  515.6 4.5 all-to-all-done.2
  520.1 5.5 all-to-all-start.5
  525.6 1.3 convolution_convert_fusion.4
  528.5 1.2 copy.118
  529.7 2.4 reshape.150
  532.1 25.7 %all-to-all-done.5 = bf16[64,320,20]{1,2,0:T(8,128)(2,1)} async-done(((bf16[64,320,20]{1,2,0:T(8,128)(2,1)}), bf16[64,320,20]{1,2,0:T(8,128)(2,1)}, u32[]{:S(2)}, u32[]{:S(2)}) %all-to-all-start.5) | async-done | bytes 819232 | tf_op jit(solution)/shard_map/all_to_all | solution.py:67
  557.8 7.1 all-to-all-start.3
  565.0 3.0 pad_maximum_fusion
  568.0 5.7 copy.120
  573.7 6.1 reshape.138
  579.7 12.4 %all-to-all-start.4 = ((bf16[64,20,1280]{2,1,0:T(8,128)(2,1)}), bf16[64,20,1280]{2,1,0:T(8,128)(2,1)}, u32[]{:S(2)}, u32[]{:S(2)}) async-start(bf16[64,20,1280]{2,1,0:T(8,128)(2,1)} %reshape.138), calls=%async_computation.4 | async-start | bytes 7864320 | tf_op jit(solution)/shard_map/all_to_all | solution.py:67
  592.8 16.2 %psum.35 = f32[]{:T(128)} all-reduce(f32[]{:T(128)S(6)} %div.89), channel_id=1, replica_groups=mesh['dp_0'=4,'dp_1'=4,'dp_2'=4,'mp_0'=2,'mp_1'=2] {'dp_0'}, use_global_device_ids=true, to_apply=%region_7.8 | all-reduce | flops 1 | bytes 8 | tf_op jit(solution)/shard_map/psum | solution.py:52
  609.0 68.8 %psum.36 = f32[]{:T(128)} all-reduce(f32[]{:T(128)} %psum.35), channel_id=1, replica_groups=mesh['dp_0'=4,'dp_1'=4,'dp_2'=4,'mp_0'=2,'mp_1'=2] {'dp_1'}, use_global_device_ids=true, to_apply=%region_8.9 | all-reduce | flops 1 | bytes 8 | tf_op jit(solution)/shard_map/psum | solution.py:52
  677.8 12.2 %psum.37 = f32[]{:T(128)} all-reduce(f32[]{:T(128)} %psum.36), channel_id=1, replica_groups=mesh['dp_0'=4,'dp_1'=4,'dp_2'=4,'mp_0'=2,'mp_1'=2] {'dp_2'}, use_global_device_ids=true, to_apply=%region_9.10 | all-reduce | flops 1 | bytes 8 | tf_op jit(solution)/shard_map/psum | solution.py:52
  690.0 4.4 psum.38
  694.4 7.3 %psum.39 = f32[]{:T(128)} all-reduce(f32[]{:T(128)} %psum.38), channel_id=1, replica_groups=mesh['dp_0'=4,'dp_1'=4,'dp_2'=4,'mp_0'=2,'mp_1'=2] {'mp_1'}, use_global_device_ids=true, to_apply=%region_11.12 | all-reduce | flops 1 | bytes 8 | tf_op jit(solution)/shard_map/psum | solution.py:52
  702.4 2.1 convert_reduce_fusion.3
  707.2 2.8 convert_reduce_fusion
  (142 shorter events, 21.7 us)
Async XLA Ops:
  7.2 344.3 %all-gather.5.cloned.1.call-start = ((), (), s32[]{:S(2)}) async-start(), calls=%async_computation.6 | async-start | bytes 3993600 | tf_op jit(solution)/shard_map/all_gather | solution.py:38
  11.4 339.6 %copy-start.11 = (bf16[128,32]{1,0:T(8,128)(2,1)}, bf16[128,32]{1,0:T(8,128)(2,1)S(1)}, u32[]{:S(2)}) copy-start(bf16[128,32]{1,0:T(8,128)(2,1)S(1)} %convert_element_type.104) | copy-start | bytes 24580
  350.6 14.3 %copy-start = (bf16[1280,320]{1,0:T(8,128)(2,1)}, bf16[1280,320]{1,0:T(8,128)(2,1)S(1)}, u32[]{:S(2)}) copy-start(bf16[1280,320]{1,0:T(8,128)(2,1)S(1)} %reshape.145) | copy-start | bytes 2457604
  351.3 6.4 copy-start.21
  351.4 10.3 %copy-start.2 = (bf16[128,1280]{1,0:T(8,128)(2,1)}, bf16[128,1280]{1,0:T(8,128)(2,1)S(1)}, u32[]{:S(2)}) copy-start(bf16[128,1280]{1,0:T(8,128)(2,1)S(1)} %multiply_convert_fusion.1) | copy-start | bytes 983044
  363.7 0.8 copy-start.9
  363.9 3.1 copy-start.15
  364.2 2.9 copy-start.17
  364.5 2.6 copy-start.25
  364.9 2.2 copy-start.6
  367.1 59.2 %copy-start.23 = (f32[8,128]{1,0:T(8,128)S(1)}, f32[8,128]{1,0:T(8,128)}, u32[]{:S(2)}) copy-start(f32[8,128]{1,0:T(8,128)} %param.10) | copy-start | bytes 12292
  367.1 87.9 %all-to-all-start = ((f32[4,128,1280]{2,1,0:T(8,128)}), f32[4,128,1280]{2,1,0:T(8,128)S(1)}, u32[]{:S(2)}, u32[]{:S(2)}) async-start(f32[4,128,1280]{2,1,0:T(8,128)} %broadcast_in_dim.61), calls=%async_computation | async-start | bytes 5242880 | tf_op jit(solution)/shard_map/all_to_all | solution.py:43
  428.8 28.4 %copy-start.13 = (f32[128,320]{0,1:T(8,128)S(1)}, f32[128,320]{0,1:T(8,128)}, u32[]{:S(2)}) copy-start(f32[128,320]{0,1:T(8,128)} %sub.62) | copy-start | bytes 491524
  428.8 28.4 %copy-start.20 = (f32[320]{0:T(512)S(1)}, f32[320]{0:T(512)}, u32[]{:S(2)}) copy-start(f32[320]{0:T(512)} %mul.236) | copy-start | bytes 3844
  428.8 28.4 %copy-start.24 = (pred[320]{0:T(512)(128)(4,1)S(1)}, pred[320]{0:T(512)(128)(4,1)}, u32[]{:S(2)}) copy-start(pred[320]{0:T(512)(128)(4,1)} %broadcast_in_dim.30) | copy-start | bytes 964
  460.2 3.2 copy-start.14
  460.2 8.8 %copy-start.26 = (f32[8,4,16,16]{2,3,1,0:T(8,128)S(1)}, f32[8,4,16,16]{2,3,1,0:T(8,128)}, u32[]{:S(2)}) copy-start(f32[8,4,16,16]{2,3,1,0:T(8,128)} %copy-done.25) | copy-start | bytes 98308
  463.4 21.9 %all-to-all-start.1 = ((bf16[4,128,1280]{2,1,0:T(8,128)(2,1)}), bf16[4,128,1280]{2,1,0:T(8,128)(2,1)}, u32[]{:S(2)}, u32[]{:S(2)}) async-start(bf16[4,128,1280]{2,1,0:T(8,128)(2,1)} %broadcast_in_dim.62), calls=%async_computation.1 | async-start | bytes 2621440 | tf_op jit(solution)/shard_map/all_to_all | solution.py:43
  468.9 18.4 %copy-start.1 = (bf16[1280,320]{1,0:T(8,128)(2,1)S(1)}, bf16[1280,320]{1,0:T(8,128)(2,1)}, u32[]{:S(2)}) copy-start(bf16[1280,320]{1,0:T(8,128)(2,1)} %copy-done) | copy-start | bytes 2457604
  469.7 18.4 %copy-start.10 = (bf16[8,16,4,80]{3,2,1,0:T(4,128)(2,1)S(1)}, bf16[8,16,4,80]{3,2,1,0:T(4,128)(2,1)}, u32[]{:S(2)}) copy-start(bf16[8,16,4,80]{3,2,1,0:T(4,128)(2,1)} %copy-done.9) | copy-start | bytes 245764
  486.9 1.5 copy-start.16
  486.9 2.7 copy-start.18
  492.4 5.6 copy-start.7
  499.1 20.9 %all-to-all-start.2 = ((bf16[4,128,1280]{2,1,0:T(8,128)(2,1)}), bf16[4,128,1280]{2,1,0:T(8,128)(2,1)S(1)}, u32[]{:S(2)}, u32[]{:S(2)}) async-start(bf16[4,128,1280]{2,1,0:T(8,128)(2,1)} %broadcast_in_dim.63), calls=%async_computation.2 | async-start | bytes 2621440 | tf_op jit(solution)/shard_map/all_to_all | solution.py:43
  506.1 6.9 copy-start.3
  510.7 14.8 %copy-start.8 = (bf16[128,320]{1,0:T(8,128)(2,1)S(1)}, bf16[128,320]{1,0:T(8,128)(2,1)}, u32[]{:S(2)}) copy-start(bf16[128,320]{1,0:T(8,128)(2,1)} %copy-done.7) | copy-start | bytes 245764
  514.3 12.8 %copy-start.22 = (f32[128]{0:T(128)S(1)}, f32[128]{0:T(128)}, u32[]{:S(2)}) copy-start(f32[128]{0:T(128)} %copy-done.21) | copy-start | bytes 1540
  520.1 37.8 %all-to-all-start.5 = ((bf16[64,320,20]{1,2,0:T(8,128)(2,1)}), bf16[64,320,20]{1,2,0:T(8,128)(2,1)}, u32[]{:S(2)}, u32[]{:S(2)}) async-start(bf16[64,320,20]{1,2,0:T(8,128)(2,1)} %bitcast.55), calls=%async_computation.5 | async-start | bytes 2359296 | tf_op jit(solution)/shard_map/all_to_all | solution.py:67
  526.9 1.1 copy-start.12
  527.5 37.5 %copy-start.4 = (bf16[1280,320]{0,1:T(8,128)(2,1)S(1)}, bf16[1280,320]{0,1:T(8,128)(2,1)}, u32[]{:S(2)}) copy-start(bf16[1280,320]{0,1:T(8,128)(2,1)} %convolution_convert_fusion.2) | copy-start | bytes 2457604
  527.7 37.3 %copy-start.5 = (bf16[1280,320]{0,1:T(8,128)(2,1)S(1)}, bf16[1280,320]{0,1:T(8,128)(2,1)}, u32[]{:S(2)}) copy-start(bf16[1280,320]{0,1:T(8,128)(2,1)} %convolution_convert_fusion.3) | copy-start | bytes 2457604
  557.8 21.9 %all-to-all-start.3 = ((f32[64,1,680]{2,1,0:T(1,128)}), f32[64,1,680]{2,1,0:T(1,128)S(1)}, u32[]{:S(2)}, u32[]{:S(2)}) async-start(f32[64,1,680]{2,1,0:T(1,128)} %reshape.150), calls=%async_computation.3 | async-start | bytes 393216 | tf_op jit(solution)/shard_map/all_to_all | solution.py:82
  579.7 127.5 %all-to-all-start.4 = ((bf16[64,20,1280]{2,1,0:T(8,128)(2,1)}), bf16[64,20,1280]{2,1,0:T(8,128)(2,1)}, u32[]{:S(2)}, u32[]{:S(2)}) async-start(bf16[64,20,1280]{2,1,0:T(8,128)(2,1)} %reshape.138), calls=%async_computation.4 | async-start | bytes 7864320 | tf_op jit(solution)/shard_map/all_to_all | solution.py:67
  706.5 4.2 copy-start.19
Sparse Core Ops, SparseCore 0:
  11.2 90.6 all-gather.4
where the time goes:
time: 721 us; the launch traced here: 719 us
  blocking collectives  446 us (62%)
  starting transfers between devices  93.1 us (13%)
  waiting for transfers between devices  72 us (10%)
  local copies, waits for them, and re-layouts  41.5 us (6%)
  matrix products  30.4 us (4%)
  other arithmetic  18.8 us (3%)
  between operations  17.2 us (2%)
    all_gather x1, blocking collectives, gather_turned(): out, at, outs = (lax.all_gather(both, axis, axis=0, tiled=True), 0, [])  172 us
    all_gather x1, blocking collectives, per_device(): output_full = lax.all_gather(attend_exit_matrix, DP, axis=1, tiled=True)  165 us
    psum x5, blocking collectives, by_axis(): x = lax.psum(x, axis)  109 us
    all_to_all x3, starting transfers between devices, from_everyone(): lax.all_to_all(jnp.broadcast_to(x[None], (length, *x.shape)), axis, 0, 0,...  68 us
    all_to_all x3, waiting for transfers between devices, from_everyone(): lax.all_to_all(jnp.broadcast_to(x[None], (length, *x.shape)), axis, 0, 0,...  46.2 us
    all_to_all x2, waiting for transfers between devices, sum_at_owner(): tiles = lax.all_to_all(split_up(x, dim, length), axis, 0, 0, tiled=True)  25.7 us
    all_to_all x2, starting transfers between devices, sum_at_owner(): tiles = lax.all_to_all(split_up(x, dim, length), axis, 0, 0, tiled=True)  17.9 us
  transfers between devices with their start and end apart: 7, of which 4 were waited for; matrix products, arithmetic and copies ran while one was open for 7% of the time, Pallas kernels for 0%

commit v1 on v0

--- a/solution.py
+++ b/solution.py
@@ -232,7 +232,9 @@
     query_full, key_full, value_full, outlook_collected = in_one_piece(
         (asking_matrix, lookup_matrix, content_matrix, outlook_matrix), DP, 0, 1
     )
-    output_full = lax.all_gather(attend_exit_matrix, DP, axis=1, tiled=True)
+    output_full = jnp.concatenate(
+        lax.all_to_all(jnp.stack([attend_exit_matrix] * lax.axis_size(DP)), DP, 0, 0), axis=1
+    )
     residual_zero = jnp.dot(patches, embed_full, preferred_element_type=jnp.float32) + jnp.tile(
         positions(PATCHES, embed_full.shape[1]), (number, 1)
     )

time: 721 us -> 550 us (0.76)
  blocking collectives: 446 us -> 294 us
  starting transfers between devices: 93.1 us -> 77.5 us
    all_gather x1 -> x0, blocking collectives: 165 us -> none  [per_device(): output_full = lax.all_gather(attend_exit_matrix, DP, axis=1, tiled=True)]
    all_to_all x3, starting transfers between devices: 68 us -> 40.4 us  [from_everyone(): lax.all_to_all(jnp.broadcast_to(x[None], (length, *x.shape)), axis, 0, 0,...]
    all_to_all x0 -> x1, starting transfers between devices: none -> 15.1 us  [per_device(): lax.all_to_all(jnp.stack([attend_exit_matrix] * lax.axis_size(DP)), DP, 0...]
    all_gather x1, blocking collectives: 172 us -> 185 us  [gather_turned(): out, at, outs = (lax.all_gather(both, axis, axis=0, tiled=True), 0, [])]
  transfers between devices with their start and end apart: 7 -> 8, of which waited for: 4 -> 5; matrix products, arithmetic and copies ran while one was open for 7% -> 8% of each run, Pallas kernels for 0% -> 0%
where the time goes in v1:
time: 550 us; the launch traced here: 549 us
  blocking collectives  294 us (53%)
  starting transfers between devices  77.5 us (14%)
  waiting for transfers between devices  75.3 us (14%)
  local copies, waits for them, and re-layouts  37.9 us (7%)
  matrix products  30.4 us (6%)
  between operations  17.3 us (3%)
  other arithmetic  15.8 us (3%)
    all_gather x1, blocking collectives, gather_turned(): out, at, outs = (lax.all_gather(both, axis, axis=0, tiled=True), 0, [])  185 us
    psum x5, blocking collectives, by_axis(): x = lax.psum(x, axis)  109 us
    all_to_all x3, waiting for transfers between devices, from_everyone(): lax.all_to_all(jnp.broadcast_to(x[None], (length, *x.shape)), axis, 0, 0,...  46.5 us
    all_to_all x3, starting transfers between devices, from_everyone(): lax.all_to_all(jnp.broadcast_to(x[None], (length, *x.shape)), axis, 0, 0,...  40.4 us
    all_to_all x2, waiting for transfers between devices, sum_at_owner(): tiles = lax.all_to_all(split_up(x, dim, length), axis, 0, 0, tiled=True)  25.7 us
    all_to_all x1, starting transfers between devices, per_device(): lax.all_to_all(jnp.stack([attend_exit_matrix] * lax.axis_size(DP)), DP, 0...  15.1 us
    all_to_all x2, starting transfers between devices, sum_at_owner(): tiles = lax.all_to_all(split_up(x, dim, length), axis, 0, 0, tiled=True)  14.9 us
  transfers between devices with their start and end apart: 8, of which 5 were waited for; matrix products, arithmetic and copies ran while one was open for 8% of the time, Pallas kernels for 0%

profile of v1, /device:TPU:1, one launch (start us, length us, event | category | flops | bytes accessed | tf_op | source)
XLA Modules:
  0.0 548.6 jit_solution(373888978994468057)
XLA Ops:
  7.2 1.5 concatenate.30
  8.8 1.9 stack.2
  10.6 15.1 %all-to-all-start = ((bf16[64,320,20]{1,2,0:T(8,128)(2,1)}), bf16[64,320,20]{1,2,0:T(8,128)(2,1)S(1)}, u32[]{:S(2)}, u32[]{:S(2)}) async-start(bf16[64,320,20]{1,2,0:T(8,128)(2,1)} %stack.2), calls=%async_computation | async-start | bytes 2359296 | tf_op jit(solution)/shard_map/all_to_all | solution.py:236
  26.5 185.4 %all-gather = bf16[64,20,34]{2,1,0:T(8,128)(2,1)S(1)} all-gather(bf16[1,20,34]{2,1,0:T(8,128)(2,1)S(1)} %maximum_bitcast_fusion.1), channel_id=1, replica_groups=mesh['dp_0'=4,'dp_1'=4,'dp_2'=4,'mp_0'=2,'mp_1'=2] {'dp_0','dp_1','dp_2'}, dimensions={0}, use_global_device_ids=true | all-gather | bytes 88400 | tf_op jit(solution)/shard_map/all_gather | solution.py:24
  213.7 6.4 %reshape.153 = bf16[1280,1280]{1,0:T(8,128)(2,1)} reshape(bf16[64,20,1280]{2,1,0:T(8,128)(2,1)} %all-gather.4.cloned.1.call-done) | data formatting | bytes 6553600
  220.1 1.7 convolution_convert_fusion.13
  221.8 2.3 convolution_convert_fusion.11
  224.2 1.7 convolution_convert_fusion.12
  227.8 1.7 broadcast_in_dim.61
  229.5 30.7 %all-to-all-start.1 = ((f32[4,128,1280]{2,1,0:T(8,128)}), f32[4,128,1280]{2,1,0:T(8,128)S(1)}, u32[]{:S(2)}, u32[]{:S(2)}) async-start(f32[4,128,1280]{2,1,0:T(8,128)} %broadcast_in_dim.61), calls=%async_computation.1 | async-start | bytes 5242880 | tf_op jit(solution)/shard_map/all_to_all | solution.py:43
  264.1 26.4 %all-to-all-done.1 = f32[4,128,1280]{2,1,0:T(8,128)S(1)} async-done(((f32[4,128,1280]{2,1,0:T(8,128)}), f32[4,128,1280]{2,1,0:T(8,128)S(1)}, u32[]{:S(2)}, u32[]{:S(2)}) %all-to-all-start.1) | async-done | bytes 2621472 | tf_op jit(solution)/shard_map/all_to_all | solution.py:43
  291.6 1.2 multiply_reduce_fusion.4
  292.8 2.9 fusion.32
  295.8 2.1 convolution_convert_fusion.5
  299.0 5.2 all-to-all-start.2
  305.0 15.6 %all-to-all-done.2 = bf16[4,128,1280]{2,1,0:T(8,128)(2,1)} async-done(((bf16[4,128,1280]{2,1,0:T(8,128)(2,1)}), bf16[4,128,1280]{2,1,0:T(8,128)(2,1)}, u32[]{:S(2)}, u32[]{:S(2)}) %all-to-all-start.2) | async-done | bytes 1310752 | tf_op jit(solution)/shard_map/all_to_all | solution.py:43
  320.6 1.6 convert_reduce_fusion.2
  323.6 1.3 fusion.9
  324.9 1.3 fusion.10
  326.2 1.2 fusion.11
  327.7 1.7 fusion.16
  329.7 1.9 convolution_add_fusion.1
  331.6 1.6 fusion.1
  334.4 4.5 all-to-all-start.3
  338.9 2.3 convolution_convert_fusion
  341.3 2.2 convolution_convert_fusion.1
  343.6 2.2 copy.122
  345.8 2.2 reshape.149
  348.0 1.3 convolution_convert_fusion.2
  349.3 1.3 convolution_convert_fusion.3
  350.7 4.5 all-to-all-done.3
  355.2 5.5 %all-to-all-start.6 = ((bf16[64,320,20]{1,2,0:T(8,128)(2,1)}), bf16[64,320,20]{1,2,0:T(8,128)(2,1)}, u32[]{:S(2)}, u32[]{:S(2)}) async-start(bf16[64,320,20]{1,2,0:T(8,128)(2,1)} %bitcast.56), calls=%async_computation.6 | async-start | bytes 2359296 | tf_op jit(solution)/shard_map/all_to_all | solution.py:67
  360.7 1.3 convolution_convert_fusion.4
  364.8 2.4 reshape.158
  367.2 25.7 %all-to-all-done.6 = bf16[64,320,20]{1,2,0:T(8,128)(2,1)} async-done(((bf16[64,320,20]{1,2,0:T(8,128)(2,1)}), bf16[64,320,20]{1,2,0:T(8,128)(2,1)}, u32[]{:S(2)}, u32[]{:S(2)}) %all-to-all-start.6) | async-done | bytes 819232 | tf_op jit(solution)/shard_map/all_to_all | solution.py:67
  392.9 7.1 %all-to-all-start.4 = ((f32[64,1,680]{2,1,0:T(1,128)}), f32[64,1,680]{2,1,0:T(1,128)S(1)}, u32[]{:S(2)}, u32[]{:S(2)}) async-start(f32[64,1,680]{2,1,0:T(1,128)} %reshape.158), calls=%async_computation.4 | async-start | bytes 393216 | tf_op jit(solution)/shard_map/all_to_all | solution.py:82
  400.1 2.9 pad_maximum_fusion
  402.9 4.0 copy.121
  407.0 2.6 reshape.148
  409.5 3.0 all-to-all-done.4
  412.5 9.4 %all-to-all-start.5 = ((bf16[64,20,1280]{2,1,0:T(8,128)(2,1)}), bf16[64,20,1280]{2,1,0:T(8,128)(2,1)}, u32[]{:S(2)}, u32[]{:S(2)}) async-start(bf16[64,20,1280]{2,1,0:T(8,128)(2,1)} %reshape.148), calls=%async_computation.5 | async-start | bytes 7864320 | tf_op jit(solution)/shard_map/all_to_all | solution.py:67
  422.6 16.2 %psum.35 = f32[]{:T(128)} all-reduce(f32[]{:T(128)S(6)} %div.89), channel_id=1, replica_groups=mesh['dp_0'=4,'dp_1'=4,'dp_2'=4,'mp_0'=2,'mp_1'=2] {'dp_0'}, use_global_device_ids=true, to_apply=%region_7.8 | all-reduce | flops 1 | bytes 8 | tf_op jit(solution)/shard_map/psum | solution.py:52
  438.8 68.8 %psum.36 = f32[]{:T(128)} all-reduce(f32[]{:T(128)} %psum.35), channel_id=1, replica_groups=mesh['dp_0'=4,'dp_1'=4,'dp_2'=4,'mp_0'=2,'mp_1'=2] {'dp_1'}, use_global_device_ids=true, to_apply=%region_8.9 | all-reduce | flops 1 | bytes 8 | tf_op jit(solution)/shard_map/psum | solution.py:52
  507.6 12.3 %psum.37 = f32[]{:T(128)} all-reduce(f32[]{:T(128)} %psum.36), channel_id=1, replica_groups=mesh['dp_0'=4,'dp_1'=4,'dp_2'=4,'mp_0'=2,'mp_1'=2] {'dp_2'}, use_global_device_ids=true, to_apply=%region_9.10 | all-reduce | flops 1 | bytes 8 | tf_op jit(solution)/shard_map/psum | solution.py:52
  519.9 4.4 psum.38
  524.3 7.3 %psum.39 = f32[]{:T(128)} all-reduce(f32[]{:T(128)} %psum.38), channel_id=1, replica_groups=mesh['dp_0'=4,'dp_1'=4,'dp_2'=4,'mp_0'=2,'mp_1'=2] {'mp_1'}, use_global_device_ids=true, to_apply=%region_11.12 | all-reduce | flops 1 | bytes 8 | tf_op jit(solution)/shard_map/psum | solution.py:52
  532.3 2.1 convert_reduce_fusion.3
  537.1 2.8 convert_reduce_fusion
  (152 shorter events, 20.6 us)
Async XLA Ops:
  7.2 18.6 %copy-start.16 = (f32[8,512]{1,0:T(8,128)S(1)}, f32[8,512]{1,0:T(8,128)}, u32[]{:S(2)}) copy-start(f32[8,512]{1,0:T(8,128)} %param.9) | copy-start | bytes 49156
  7.2 19.1 %copy-start.28 = (bf16[2,20]{1,0:T(2,128)(2,1)S(1)}, bf16[2,20]{1,0:T(2,128)(2,1)}, u32[]{:S(2)}) copy-start(bf16[2,20]{1,0:T(2,128)(2,1)} %param.12) | copy-start | bytes 244
  7.2 19.2 %copy-start.23 = (bf16[32,20]{0,1:T(8,128)(2,1)S(1)}, bf16[32,20]{0,1:T(8,128)(2,1)}, u32[]{:S(2)}) copy-start(bf16[32,20]{0,1:T(8,128)(2,1)} %param.11) | copy-start | bytes 3844
  7.2 206.5 %all-gather.4.cloned.1.call-start = ((), (), s32[]{:S(2)}) async-start(), calls=%async_computation.7 | async-start | bytes 3993600 | tf_op jit(solution)/shard_map/all_gather | solution.py:38
  10.6 202.6 %all-to-all-start = ((bf16[64,320,20]{1,2,0:T(8,128)(2,1)}), bf16[64,320,20]{1,2,0:T(8,128)(2,1)S(1)}, u32[]{:S(2)}, u32[]{:S(2)}) async-start(bf16[64,320,20]{1,2,0:T(8,128)(2,1)} %stack.2), calls=%async_computation | async-start | bytes 2359296 | tf_op jit(solution)/shard_map/all_to_all | solution.py:236
  26.3 186.8 %copy-start.12 = (bf16[128,32]{1,0:T(8,128)(2,1)}, bf16[128,32]{1,0:T(8,128)(2,1)S(1)}, u32[]{:S(2)}) copy-start(bf16[128,32]{1,0:T(8,128)(2,1)S(1)} %convert_element_type.104) | copy-start | bytes 24580
  213.0 7.1 %copy-start.24 = (f32[128]{0:T(128)}, f32[128]{0:T(128)S(1)}, u32[]{:S(2)}) copy-start(f32[128]{0:T(128)S(1)} %add_rsqrt_fusion.1) | copy-start | bytes 1540
  213.2 11.0 %copy-start.2 = (bf16[128,1280]{1,0:T(8,128)(2,1)}, bf16[128,1280]{1,0:T(8,128)(2,1)S(1)}, u32[]{:S(2)}) copy-start(bf16[128,1280]{1,0:T(8,128)(2,1)S(1)} %multiply_convert_fusion.1) | copy-start | bytes 983044
  213.6 13.7 %copy-start = (bf16[320,1280]{0,1:T(8,128)(2,1)}, bf16[320,1280]{0,1:T(8,128)(2,1)S(1)}, u32[]{:S(2)}) copy-start(bf16[320,1280]{0,1:T(8,128)(2,1)S(1)} %reshape.143) | copy-start | bytes 2457604
  226.1 0.8 copy-start.10
  226.4 3.1 copy-start.17
  226.7 2.9 copy-start.19
  226.9 2.6 copy-start.29
  227.4 2.2 copy-start.7
  229.5 32.1 %copy-start.26 = (f32[8,128]{1,0:T(8,128)S(1)}, f32[8,128]{1,0:T(8,128)}, u32[]{:S(2)}) copy-start(f32[8,128]{1,0:T(8,128)} %param.10) | copy-start | bytes 12292
  229.5 61.0 %all-to-all-start.1 = ((f32[4,128,1280]{2,1,0:T(8,128)}), f32[4,128,1280]{2,1,0:T(8,128)S(1)}, u32[]{:S(2)}, u32[]{:S(2)}) async-start(f32[4,128,1280]{2,1,0:T(8,128)} %broadcast_in_dim.61), calls=%async_computation.1 | async-start | bytes 5242880 | tf_op jit(solution)/shard_map/all_to_all | solution.py:43
  264.1 28.7 %copy-start.14 = (f32[128,320]{0,1:T(8,128)S(1)}, f32[128,320]{0,1:T(8,128)}, u32[]{:S(2)}) copy-start(f32[128,320]{0,1:T(8,128)} %sub.62) | copy-start | bytes 491524
  264.1 28.7 %copy-start.22 = (f32[320]{0:T(512)S(1)}, f32[320]{0:T(512)}, u32[]{:S(2)}) copy-start(f32[320]{0:T(512)} %mul.236) | copy-start | bytes 3844
  264.1 28.7 %copy-start.27 = (pred[320]{0:T(512)(128)(4,1)S(1)}, pred[320]{0:T(512)(128)(4,1)}, u32[]{:S(2)}) copy-start(pred[320]{0:T(512)(128)(4,1)} %broadcast_in_dim.30) | copy-start | bytes 964
  295.8 3.2 copy-start.15
  295.8 8.5 %copy-start.30 = (f32[8,4,16,16]{2,3,1,0:T(8,128)S(1)}, f32[8,4,16,16]{2,3,1,0:T(8,128)}, u32[]{:S(2)}) copy-start(f32[8,4,16,16]{2,3,1,0:T(8,128)} %copy-done.29) | copy-start | bytes 98308
  299.0 21.6 %all-to-all-start.2 = ((bf16[4,128,1280]{2,1,0:T(8,128)(2,1)}), bf16[4,128,1280]{2,1,0:T(8,128)(2,1)}, u32[]{:S(2)}, u32[]{:S(2)}) async-start(bf16[4,128,1280]{2,1,0:T(8,128)(2,1)} %broadcast_in_dim.62), calls=%async_computation.2 | async-start | bytes 2621440 | tf_op jit(solution)/shard_map/all_to_all | solution.py:43
  304.2 18.4 %copy-start.1 = (bf16[320,1280]{0,1:T(8,128)(2,1)S(1)}, bf16[320,1280]{0,1:T(8,128)(2,1)}, u32[]{:S(2)}) copy-start(bf16[320,1280]{0,1:T(8,128)(2,1)} %copy-done) | copy-start | bytes 2457604
  305.0 18.4 %copy-start.11 = (bf16[8,16,4,80]{3,2,1,0:T(4,128)(2,1)S(1)}, bf16[8,16,4,80]{3,2,1,0:T(4,128)(2,1)}, u32[]{:S(2)}) copy-start(bf16[8,16,4,80]{3,2,1,0:T(4,128)(2,1)} %copy-done.10) | copy-start | bytes 245764
  322.2 1.5 copy-start.18
  322.2 2.7 copy-start.20
  327.7 5.6 %copy-start.8 = (bf16[128,320]{1,0:T(8,128)(2,1)}, bf16[128,320]{1,0:T(8,128)(2,1)S(1)}, u32[]{:S(2)}) copy-start(bf16[128,320]{1,0:T(8,128)(2,1)S(1)} %reshape.145) | copy-start | bytes 245764
  334.4 20.8 %all-to-all-start.3 = ((bf16[4,128,1280]{2,1,0:T(8,128)(2,1)}), bf16[4,128,1280]{2,1,0:T(8,128)(2,1)S(1)}, u32[]{:S(2)}, u32[]{:S(2)}) async-start(bf16[4,128,1280]{2,1,0:T(8,128)(2,1)} %broadcast_in_dim.63), calls=%async_computation.3 | async-start | bytes 2621440 | tf_op jit(solution)/shard_map/all_to_all | solution.py:43
  341.2 6.9 %copy-start.3 = (bf16[128,1280]{1,0:T(8,128)(2,1)S(1)}, bf16[128,1280]{1,0:T(8,128)(2,1)}, u32[]{:S(2)}) copy-start(bf16[128,1280]{1,0:T(8,128)(2,1)} %copy-done.2) | copy-start | bytes 983044
  345.8 14.8 %copy-start.9 = (bf16[128,320]{1,0:T(8,128)(2,1)S(1)}, bf16[128,320]{1,0:T(8,128)(2,1)}, u32[]{:S(2)}) copy-start(bf16[128,320]{1,0:T(8,128)(2,1)} %copy-done.8) | copy-start | bytes 245764
  349.3 12.8 %copy-start.25 = (f32[128]{0:T(128)S(1)}, f32[128]{0:T(128)}, u32[]{:S(2)}) copy-start(f32[128]{0:T(128)} %copy-done.24) | copy-start | bytes 1540
  355.2 37.8 %all-to-all-start.6 = ((bf16[64,320,20]{1,2,0:T(8,128)(2,1)}), bf16[64,320,20]{1,2,0:T(8,128)(2,1)}, u32[]{:S(2)}, u32[]{:S(2)}) async-start(bf16[64,320,20]{1,2,0:T(8,128)(2,1)} %bitcast.56), calls=%async_computation.6 | async-start | bytes 2359296 | tf_op jit(solution)/shard_map/all_to_all | solution.py:67
  362.0 1.1 copy-start.13
  362.5 37.5 %copy-start.4 = (bf16[1280,320]{0,1:T(8,128)(2,1)S(1)}, bf16[1280,320]{0,1:T(8,128)(2,1)}, u32[]{:S(2)}) copy-start(bf16[1280,320]{0,1:T(8,128)(2,1)} %convolution_convert_fusion.2) | copy-start | bytes 2457604
  362.8 37.3 %copy-start.5 = (bf16[1280,320]{0,1:T(8,128)(2,1)S(1)}, bf16[1280,320]{0,1:T(8,128)(2,1)}, u32[]{:S(2)}) copy-start(bf16[1280,320]{0,1:T(8,128)(2,1)} %convolution_convert_fusion.3) | copy-start | bytes 2457604
  362.8 37.3 %copy-start.6 = (bf16[1280,320]{0,1:T(8,128)(2,1)S(1)}, bf16[1280,320]{0,1:T(8,128)(2,1)}, u32[]{:S(2)}) copy-start(bf16[1280,320]{0,1:T(8,128)(2,1)} %convolution_convert_fusion.4) | copy-start | bytes 2457604
  392.9 19.6 %all-to-all-start.4 = ((f32[64,1,680]{2,1,0:T(1,128)}), f32[64,1,680]{2,1,0:T(1,128)S(1)}, u32[]{:S(2)}, u32[]{:S(2)}) async-start(f32[64,1,680]{2,1,0:T(1,128)} %reshape.158), calls=%async_computation.4 | async-start | bytes 393216 | tf_op jit(solution)/shard_map/all_to_all | solution.py:82
  412.5 124.6 %all-to-all-start.5 = ((bf16[64,20,1280]{2,1,0:T(8,128)(2,1)}), bf16[64,20,1280]{2,1,0:T(8,128)(2,1)}, u32[]{:S(2)}, u32[]{:S(2)}) async-start(bf16[64,20,1280]{2,1,0:T(8,128)(2,1)} %reshape.148), calls=%async_computation.5 | async-start | bytes 7864320 | tf_op jit(solution)/shard_map/all_to_all | solution.py:67
  536.4 4.2 copy-start.21
Sparse Core Ops, SparseCore 0:
  11.2 96.7 all-gather.3
